TPU v7x, 32 devices: a whole 2x2x4 slice. The times are simulated.
32 devices in a mesh: row: 4 (over y, core), col: 8 (over z, x).
Axes of the slice: x: 2, y: 2, z: 4, core: 2. Of those that a mesh axis runs over, the one named last changes fastest.
Arguments:
- volume: float32 [8, 1024, 1024], P(None, 'row', 'col'), may hold values from -6 to 6
- ray_weights: float32 [16, 1024], P(None, 'row'), may hold values from 0.5 to 2
- shear_weights: bfloat16 [16, 128, 128], replicated, may hold values from -0.5 to 0.5
- shear_offsets: int32 [16], replicated, may hold values from 0 to 7
- measured: float32 [16, 8, 1024], P('row', None, 'col'), may hold values from -6 to 6
Outputs:
- residual: float32 [16, 8, 1024], P('row', None, 'col')
- gradient: float32 [8, 1024, 1024], P(None, 'row', 'col')
All inputs are finite; a program needn't handle non-finite values.
Results may differ from a plain program's by a relative error of at most 0.0003.
Values sent between devices are 32-bit elements; how exact they have to be, the bound alone decides.
A program may use at most 64 MiB of HBM per device.

v0:
```python
import functools
import math

import jax
import jax.numpy as jnp
from jax import lax
from jax.experimental import pallas as pl
from jax.experimental.pallas import tpu as pltpu
from jax.sharding import PartitionSpec as P

MESH = pl.DeviceIdType.MESH
UNROLL_UP_TO = 64
KERNEL_VMEM = 24 * 1024 * 1024


def split(value):
    high = value.astype(jnp.bfloat16)
    return high, (value - high.astype(jnp.float32)).astype(jnp.bfloat16)


def each(count, body):
    if count <= UNROLL_UP_TO:
        for step in range(count):
            body(step)
    else:
        lax.fori_loop(0, count, lambda step, _: (body(step), 0)[1], 0)


def flip(index, step, size):
    if size & (size - 1):
        return lax.rem(index + step, size)
    bit = 1
    while bit < size:
        if step & bit:
            index = index + bit - 2 * bit * lax.rem(index // bit, 2)
        bit *= 2
    return index


def far_first(size):
    quarter = max(size // 4, 1)
    place = {2: 0, 3: 1, 1: 2, 0: 3}
    return sorted(range(size), key=lambda step: (place.get(step // quarter, 2), -step))


def bytes_of(ref, blocks, sem):
    part = ref.at[pl.ds(0, blocks)]
    return pltpu.make_async_copy(part, part, sem)


def exchange(
    rows, cols, factor,
    volume_ref, weights_ref, shear_ref, offsets_ref, measured_ref,
    columns_ref, spread_ref, residual_ref,
    slab, weights_in, shear, offsets, measured, sums, tiles, landed, measure_in, resid, pulls, pulled, resid_in,
    slab_sem, local_sem, out_sem, in_sem, back_out_sem, back_in_sem, m_out_sem, m_in_sem, r_out_sem, r_in_sem,
):
    slices = volume_ref.shape[0]
    angles = weights_ref.shape[0]
    owned = measured_ref.shape[0]
    base = (cols - owned) // 2
    count = rows * cols
    row, col = lax.axis_index("row"), lax.axis_index("col")
    me = row * cols + col
    at_home = jnp.logical_and(col >= base, col < base + owned)
    away = jnp.logical_not(at_home)
    mine = row * owned + lax.clamp(0, col - base, owned - 1)

    def home(angle):
        return angle // owned, base + lax.rem(angle, owned)

    unrolled = count <= UNROLL_UP_TO
    other_rows = [flip(row, step, rows) for step in reversed(range(rows))] if unrolled else None
    other_cols = [flip(col, step, cols) for step in far_first(cols)] if unrolled else None
    near = lax.clamp(0, col - base, owned - 1)
    other_places = [flip(near, step, owned) for step in far_first(owned)] if unrolled else None

    def peer(step):
        if unrolled:
            target = other_rows[step % rows], other_cols[step // rows]
            return target[0] * cols + target[1], target
        other = lax.rem(me + step + 1, count)
        return other, (other // cols, lax.rem(other, cols))

    def signal(device):
        pl.semaphore_signal(barrier, inc=1, device_id=device, device_id_type=MESH)

    barrier = pltpu.get_barrier_semaphore()

    @pl.when(at_home)
    def _():
        each(count - 1, lambda step: signal(peer(step)[1]))

    weights_copy = pltpu.make_async_copy(weights_ref, weights_in, local_sem.at[0])
    weights_copy.start()
    volume_copies = []
    for s in range(slices):
        copy = pltpu.make_async_copy(volume_ref.at[s], slab.at[s], slab_sem.at[s])
        copy.start()
        volume_copies.append(copy)
    shear_copy = pltpu.make_async_copy(shear_ref, shear, local_sem.at[1])
    shear_copy.start()
    measured_copy = pltpu.make_async_copy(measured_ref, measured, local_sem.at[2])
    measured_copy.start()
    offsets_copy = pltpu.make_async_copy(offsets_ref, offsets, local_sem.at[3])
    offsets_copy.start()

    @pl.when(away)
    def _():
        each(angles, lambda angle: signal(home(angle)))

    weights_copy.wait()
    weights = weights_in[...] * factor
    w_high, w_low = split(weights)
    w_both = jnp.concatenate([w_high, w_low], axis=0)
    for s in range(slices):
        volume_copies[s].wait()
        v_high, v_low = split(slab[s])
        first = jnp.dot(w_both, v_high, preferred_element_type=jnp.float32)
        second = jnp.dot(w_high, v_low, preferred_element_type=jnp.float32)
        sums[pl.ds(s, angles, stride=slices), :] = first[:angles] + first[angles:] + second
    shear_copy.wait()
    for a in range(angles):
        t_high, t_low = split(sums[a * slices:(a + 1) * slices, :])
        both = jnp.dot(jnp.concatenate([t_high, t_low], axis=0), shear[a], preferred_element_type=jnp.float32)
        tiles[a] = both[:slices] + both[slices:]
    measured_copy.wait()
    offsets_copy.wait()

    @pl.when(at_home)
    def _():
        pl.semaphore_wait(barrier, count - 1)

    @pl.when(away)
    def _():
        pl.semaphore_wait(barrier, angles)

    def send(source, target, send_sem, recv_sem, device):
        pltpu.make_async_remote_copy(
            src_ref=source, dst_ref=target, send_sem=send_sem, recv_sem=recv_sem,
            device_id=device, device_id_type=MESH).start()

    def send_measured(step):
        place = other_places[step] if unrolled else lax.rem(lax.select(at_home, col - base + 1, 0) + step, owned)
        send(measured.at[place], measure_in.at[col], m_out_sem, m_in_sem, (row, base + place))

    def send_tile(step):
        if unrolled:
            target, place = other_rows[step % rows], other_places[step // rows]
            send(tiles.at[target * owned + place], landed.at[me], out_sem, in_sem, (target, base + place))
            return
        angle = lax.rem(lax.select(at_home, mine + 1, row * owned) + step, angles)
        send(tiles.at[angle], landed.at[me], out_sem, in_sem, home(angle))

    each(angles - 1, send_tile)
    each(owned - 1, send_measured)

    @pl.when(away)
    def _():
        send_measured(owned - 1)
        send_tile(angles - 1)

    columns_ref[...] = jnp.concatenate(
        [weights, weights - w_high.astype(jnp.float32), weights], axis=0).T.astype(jnp.bfloat16)

    @pl.when(at_home)
    def _():
        landed[me] = tiles[mine]
        measure_in[col] = measured[col - base]
        offset = offsets[mine]
        bytes_of(measure_in, cols - 1, m_in_sem).wait()
        bytes_of(landed, count - 1, in_sem).wait()
        for c in range(cols):
            total = landed[c]
            for r in range(1, rows):
                total = total + landed[r * cols + lax.rem((cols - offset) * r + c, cols)]
            resid[c] = total - measure_in[c]
        for r in range(rows):
            for c in range(cols):
                pulls[r * cols + c] = resid[lax.rem(offset * r + c, cols)]

        def send_pull(step):
            other, device = peer(step)
            send(pulls.at[other], pulled.at[mine], back_out_sem, back_in_sem, device)

        def send_resid(step):
            other = other_cols[step] if unrolled else lax.rem(col + step + 1, cols)
            send(resid.at[other], resid_in.at[col - base], r_out_sem, r_in_sem, (row, other))

        each(count - 1, send_pull)
        each(cols - 1, send_resid)
        pulled[mine] = pulls[me]
        resid_in[col - base] = resid[col]
        bytes_of(pulled, angles - 1, back_in_sem).wait()

    @pl.when(away)
    def _():
        bytes_of(pulled, angles, back_in_sem).wait()

    for a in range(angles):
        p_high, p_low = split(pulled[a])
        both = lax.dot_general(
            jnp.concatenate([p_high, p_low], axis=0), shear[a], (((1,), (1,)), ((), ())),
            preferred_element_type=jnp.float32)
        sums[a * slices:(a + 1) * slices, :] = both[:slices] + both[slices:]
    for s in range(slices):
        g_high, g_low = split(sums[pl.ds(s, angles, stride=slices), :])
        spread_ref[s] = jnp.concatenate([g_high, g_high, g_low], axis=0)

    @pl.when(at_home)
    def _():
        bytes_of(resid_in, owned - 1, r_in_sem).wait()
        bytes_of(tiles, angles - 1, out_sem).wait()
        bytes_of(measured, owned - 1, m_out_sem).wait()
        bytes_of(pulls, count - 1, back_out_sem).wait()
        bytes_of(resid, cols - 1, r_out_sem).wait()

    @pl.when(away)
    def _():
        bytes_of(resid_in, owned, r_in_sem).wait()
        bytes_of(tiles, angles, out_sem).wait()
        bytes_of(measured, owned, m_out_sem).wait()

    residual_ref[...] = resid_in[...]


def finish(columns_ref, spread_ref, resid_ref, residual_ref, gradient_ref, stage, stage_sem, resid_sem):
    copies = [pltpu.make_async_copy(resid_ref, residual_ref, resid_sem)]
    copies[0].start()
    for s in range(spread_ref.shape[0]):
        stage[s] = jnp.dot(columns_ref[...], spread_ref[s], preferred_element_type=jnp.float32)
        copy = pltpu.make_async_copy(stage.at[s], gradient_ref.at[s], stage_sem.at[s])
        copy.start()
        copies.append(copy)
    for copy in copies:
        copy.wait()


def on_device(volume, ray_weights, shear_weights, shear_offsets, measured):
    rows, cols = lax.axis_size("row"), lax.axis_size("col")
    slices, slab_rows, width = volume.shape
    angles = ray_weights.shape[0]
    owned = measured.shape[0]
    count = rows * cols
    f32, bf16 = jnp.float32, jnp.bfloat16
    dma = pltpu.SemaphoreType.DMA
    vmem = pl.BlockSpec(memory_space=pltpu.VMEM)
    hbm = pl.BlockSpec(memory_space=pltpu.HBM)

    def blocks(number):
        return pltpu.VMEM((number, slices, width), f32)

    columns, spread, resid = pl.pallas_call(
        functools.partial(exchange, rows, cols, 1.0 / math.sqrt(slab_rows * rows)),
        out_shape=(
            jax.ShapeDtypeStruct((slab_rows, 3 * angles), bf16),
            jax.ShapeDtypeStruct((slices, 3 * angles, width), bf16),
            jax.ShapeDtypeStruct(measured.shape, f32)),
        in_specs=[hbm] * 5,
        out_specs=(vmem, vmem, vmem),
        scratch_shapes=[
            pltpu.VMEM(volume.shape, f32),
            pltpu.VMEM(ray_weights.shape, f32),
            pltpu.VMEM(shear_weights.shape, shear_weights.dtype),
            pltpu.SMEM(shear_offsets.shape, jnp.int32),
            blocks(owned),
            pltpu.VMEM((angles * slices, width), f32),
            blocks(angles), blocks(count), blocks(cols), blocks(cols), blocks(count), blocks(angles), blocks(owned),
            dma((slices,)), dma((4,)), dma, dma, dma, dma, dma, dma, dma, dma,
        ],
        compiler_params=pltpu.CompilerParams(collective_id=0, has_side_effects=True, vmem_limit_bytes=KERNEL_VMEM),
        name="exchange",
    )(*(pltpu.with_memory_space_constraint(value, pltpu.HBM)
        for value in (volume, ray_weights, shear_weights, shear_offsets, measured)))
    return pl.pallas_call(
        finish,
        out_shape=(jax.ShapeDtypeStruct(measured.shape, f32), jax.ShapeDtypeStruct(volume.shape, f32)),
        in_specs=[vmem] * 3,
        out_specs=(hbm, hbm),
        scratch_shapes=[pltpu.VMEM(volume.shape, f32), dma((slices,)), dma],
        compiler_params=pltpu.CompilerParams(vmem_limit_bytes=KERNEL_VMEM),
        name="finish",
    )(columns, spread, resid)


def solution(mesh):
    placed = (P(None, "row", "col"), P(None, "row"), P(), P(), P("row", None, "col"))
    return jax.shard_map(
        on_device,
        mesh=mesh,
        in_specs=placed,
        out_specs=(P("row", None, "col"), P(None, "row", "col")),
        check_vma=False,
    )
```

profile of v0, /device:TPU:0, one launch (start us, length us, event | category | flops | bytes accessed | tf_op | source)
XLA Modules:
  0.0 17.4 jit_solution(552246222831545616)
XLA Ops:
  0.6 15.6 %exchange.1 = (bf16[256,48]{1,0:T(8,128)(2,1)S(1)}, bf16[8,48,128]{2,1,0:T(8,128)(2,1)S(1)}, f32[4,8,128]{2,1,0:T(8,128)S(1)}) custom-call(f32[8,256,128]{2,1,0:T(8,128)} %volume_ref.1, f32[16,256]{1,0:T(8,128)} %weights_ref.1, bf16[16,128,128]{2,1,0:T(8,128)(2,1)} %shear_ref.1, s32[16]{0:T(128)} %offsets_ref.1, f32[4,8,128]{2,1,0:T(8,128)} %measured_ref.1), custom_call_target="tpu_custom_call" | custom-call | tf_op jit(solution)/shard_map/exchange/pallas_call | solution.py:253
  16.2 1.2 %finish.1 = (f32[4,8,128]{2,1,0:T(8,128)}, f32[8,256,128]{2,1,0:T(8,128)}) custom-call(bf16[256,48]{1,0:T(8,128)(2,1)S(1)} %get-tuple-element.5.columns_ref, bf16[8,48,128]{2,1,0:T(8,128)(2,1)S(1)} %get-tuple-element.6.spread_ref, f32[4,8,128]{2,1,0:T(8,128)S(1)} %get-tuple-element.7.resid_ref), custom_call_target="tpu_custom_call" | custom-call | tf_op jit(solution)/shard_map/finish/pallas_call | solution.py:275
where the time goes:
time: 17.5 us; the launch traced here: 17.4 us
  Pallas kernels  16.8 us (96%)
  between operations  0.64 us (4%)
    pallas_call x1, Pallas kernels, on_device(): pl.pallas_call(functools.partial(exchange, rows, cols, 1.0 / math.sqrt(sl...  15.6 us
    pallas_call x1, Pallas kernels, on_device(): pl.pallas_call(finish, out_shape=(jax.ShapeDtypeStruct(measured.shape, f3...  1.2 us

commit v1 on v0

v1 whole, which is shorter than its diff:
```python
import functools
import math

import jax
import jax.numpy as jnp
from jax import lax
from jax.experimental import pallas as pl
from jax.experimental.pallas import tpu as pltpu
from jax.sharding import PartitionSpec as P

MESH = pl.DeviceIdType.MESH
UNROLL_UP_TO = 64
KERNEL_VMEM = 24 * 1024 * 1024


def split(value):
    high = value.astype(jnp.bfloat16)
    return high, (value - high.astype(jnp.float32)).astype(jnp.bfloat16)


def each(count, body):
    if count <= UNROLL_UP_TO:
        for step in range(count):
            body(step)
    else:
        lax.fori_loop(0, count, lambda step, _: (body(step), 0)[1], 0)


def flip(index, step, size):
    if size & (size - 1):
        return lax.rem(index + step, size)
    bit = 1
    while bit < size:
        if step & bit:
            index = index + bit - 2 * bit * lax.rem(index // bit, 2)
        bit *= 2
    return index


def far_first(size):
    return sorted(range(1, size), key=lambda step: (-step.bit_count(), -step)) + [0]


def bytes_of(ref, blocks, sem):
    part = ref.at[pl.ds(0, blocks)]
    return pltpu.make_async_copy(part, part, sem)


class Homes:
    def __init__(self, rows, cols, angles):
        owned = angles // rows
        self.group = 2 if rows % 2 == 0 and owned % 2 == 0 else 1
        self.per = 2 if owned % 2 == 0 else 1
        self.beside = self.group * owned // self.per
        self.count = angles // self.per
        self.owned = owned
        self.base = (cols - self.beside) // 2

    def place(self, home):
        return home // self.beside * self.group + self.group - 1, self.base + lax.rem(home, self.beside)

    def owner(self, home):
        return home * self.per // self.owned


def exchange(
    rows, cols, factor, homes,
    volume_ref, weights_ref, shear_ref, offsets_ref, measured_ref,
    columns_ref, spread_ref, residual_ref,
    slab, weights_in, shear, offsets, measured, tiles, landed, measure_in, resid, spreads, pulls, pulled, resid_in,
    slab_sem, local_sem, out_sem, in_sem, back_out_sem, back_in_sem, m_out_sem, m_in_sem, r_out_sem, r_in_sem,
):
    slices = volume_ref.shape[0]
    angles = weights_ref.shape[0]
    owned = measured_ref.shape[0]
    width = volume_ref.shape[2]
    per, base, beside = homes.per, homes.base, homes.beside
    own_homes = owned // per
    count = rows * cols
    row, col = lax.axis_index("row"), lax.axis_index("col")
    me = row * cols + col
    at_home = jnp.logical_and(
        lax.rem(row, homes.group) == homes.group - 1, jnp.logical_and(col >= base, col < base + beside))
    away = jnp.logical_not(at_home)
    mine = row // homes.group * beside + lax.clamp(0, col - base, beside - 1)
    owner = homes.owner(mine)
    owner_here = jnp.logical_and(at_home, owner == row)
    owner_there = jnp.logical_and(at_home, owner != row)

    def device(index):
        return index // cols, lax.rem(index, cols)

    def others(body):
        if count <= UNROLL_UP_TO:
            for index in sorted(range(count), key=lambda index: (index % cols, index // cols)):
                pl.when(me != index)(functools.partial(body, index, (index // cols, index % cols)))
        else:
            def step(offset, carry):
                other = lax.rem(me + offset, count)
                body(other, device(other))
                return carry
            lax.fori_loop(1, count, step, 0)

    barrier = pltpu.get_barrier_semaphore()

    weights_copy = pltpu.make_async_copy(weights_ref, weights_in, local_sem.at[0])
    weights_copy.start()
    volume_copies = []
    for s in range(slices):
        copy = pltpu.make_async_copy(volume_ref.at[s], slab.at[s], slab_sem.at[s])
        copy.start()
        volume_copies.append(copy)

    @pl.when(at_home)
    def _():
        others(lambda index, place: pl.semaphore_signal(barrier, inc=1, device_id=place, device_id_type=MESH))

    measured_copy = pltpu.make_async_copy(measured_ref, measured, local_sem.at[2])
    measured_copy.start()
    shear_copy = pltpu.make_async_copy(shear_ref.at[pl.ds(mine * per, per)], shear, local_sem.at[1])
    shear_copy.start()
    offsets_copy = pltpu.make_async_copy(offsets_ref, offsets, local_sem.at[3])
    offsets_copy.start()

    weights_copy.wait()
    weights = weights_in[...] * factor
    w_high, w_low = split(weights)
    w_both = jnp.concatenate([w_high, w_low], axis=0)
    for s in range(slices):
        volume_copies[s].wait()
        v_high, v_low = split(slab[s])
        first = jnp.dot(w_both, v_high, preferred_element_type=jnp.float32)
        second = jnp.dot(w_high, v_low, preferred_element_type=jnp.float32)
        tiles[pl.ds(s, angles, stride=slices), :] = first[:angles] + first[angles:] + second
    measured_copy.wait()
    shear_copy.wait()
    offsets_copy.wait()

    @pl.when(at_home)
    def _():
        pl.semaphore_wait(barrier, homes.count - 1)

    @pl.when(away)
    def _():
        pl.semaphore_wait(barrier, homes.count)

    def send(source, target, send_sem, recv_sem, place):
        pltpu.make_async_remote_copy(
            src_ref=source, dst_ref=target, send_sem=send_sem, recv_sem=recv_sem,
            device_id=place, device_id_type=MESH).start()

    block = per * slices

    def send_tile(step):
        home = flip(mine, step, homes.count)
        send(tiles.at[pl.ds(home * block, block)], landed.at[me], out_sem, in_sem, homes.place(home))

    for step in far_first(homes.count)[:-1]:
        send_tile(step)
    pl.when(away)(functools.partial(send_tile, 0))

    for k in range(own_homes):
        home = row * own_homes + k
        place = homes.place(home)
        here = jnp.logical_and(place[0] == row, place[1] == col)

        @pl.when(jnp.logical_not(here))
        def _():
            send(measured.at[pl.ds(k * per, per)], measure_in.at[col], m_out_sem, m_in_sem, place)

        @pl.when(here)
        def _():
            measure_in[col] = measured[k * per:(k + 1) * per]

    columns_ref[...] = jnp.concatenate(
        [weights, weights - w_high.astype(jnp.float32), weights], axis=0).T.astype(jnp.bfloat16)

    @pl.when(at_home)
    def _():
        landed[me] = tiles[pl.ds(pl.multiple_of(mine * block, block), block), :]

    @pl.when(owner_here)
    def _():
        bytes_of(measure_in, cols - 1, m_in_sem).wait()

    @pl.when(owner_there)
    def _():
        bytes_of(measure_in, cols, m_in_sem).wait()

    @pl.when(at_home)
    def _():
        bytes_of(landed, count - 1, in_sem).wait()
        for slot in range(per):
            part = slice(slot * slices, (slot + 1) * slices)
            offset = offsets[mine * per + slot]
            totals = []
            for c in range(cols):
                total = landed[c, part]
                for r in range(1, rows):
                    total = total + landed[r * cols + lax.rem((cols - offset) * r + c, cols), part]
                totals.append(total)
            t_high, t_low = split(jnp.concatenate(totals, axis=0))
            both = jnp.dot(jnp.concatenate([t_high, t_low], axis=0), shear[slot], preferred_element_type=jnp.float32)
            line = both[:cols * slices] + both[cols * slices:]
            line = line - jnp.concatenate([measure_in[c, slot] for c in range(cols)], axis=0)
            for c in range(cols):
                resid[c, slot] = line[c * slices:(c + 1) * slices]
            l_high, l_low = split(line)
            both = lax.dot_general(
                jnp.concatenate([l_high, l_low], axis=0), shear[slot], (((1,), (1,)), ((), ())),
                preferred_element_type=jnp.float32)
            spread = both[:cols * slices] + both[cols * slices:]
            for c in range(cols):
                spreads[slot, c] = spread[c * slices:(c + 1) * slices]
            for r in range(rows):
                for c in range(cols):
                    pulls[r * cols + c, slot] = spreads[slot, lax.rem(offset * r + c, cols)]

        others(lambda index, place: send(
            pulls.at[index], pulled.at[pl.ds(mine * per, per)], back_out_sem, back_in_sem, place))
        slot = lax.rem(mine, own_homes) * per

        def send_resid(c):
            @pl.when(jnp.logical_not(jnp.logical_and(owner == row, c == col)))
            def _():
                send(resid.at[c], resid_in.at[pl.ds(slot, per)], r_out_sem, r_in_sem, (owner, c))

        each(cols, send_resid)
        pulled[pl.ds(mine * per, per)] = pulls[me]

        @pl.when(owner == row)
        def _():
            resid_in[pl.ds(slot, per)] = resid[col]

        bytes_of(pulled, angles - per, back_in_sem).wait()

    @pl.when(away)
    def _():
        bytes_of(pulled, angles, back_in_sem).wait()

    for s in range(slices):
        g_high, g_low = split(pulled[:, s, :])
        spread_ref[s] = jnp.concatenate([g_high, g_high, g_low], axis=0)

    @pl.when(owner_here)
    def _():
        bytes_of(resid_in, owned - per, r_in_sem).wait()
        bytes_of(measured, owned - per, m_out_sem).wait()
        bytes_of(resid, cols - 1, r_out_sem).wait()

    @pl.when(jnp.logical_not(owner_here))
    def _():
        bytes_of(resid_in, owned, r_in_sem).wait()
        bytes_of(measured, owned, m_out_sem).wait()

    @pl.when(owner_there)
    def _():
        bytes_of(resid, cols, r_out_sem).wait()

    @pl.when(at_home)
    def _():
        bytes_of(tiles, (homes.count - 1) * block, out_sem).wait()
        bytes_of(pulls, count - 1, back_out_sem).wait()

    @pl.when(away)
    def _():
        bytes_of(tiles, homes.count * block, out_sem).wait()

    residual_ref[...] = resid_in[...]


def finish(columns_ref, spread_ref, resid_ref, residual_ref, gradient_ref, stage, stage_sem, resid_sem):
    copies = [pltpu.make_async_copy(resid_ref, residual_ref, resid_sem)]
    copies[0].start()
    for s in range(spread_ref.shape[0]):
        stage[s] = jnp.dot(columns_ref[...], spread_ref[s], preferred_element_type=jnp.float32)
        copy = pltpu.make_async_copy(stage.at[s], gradient_ref.at[s], stage_sem.at[s])
        copy.start()
        copies.append(copy)
    for copy in copies:
        copy.wait()


def on_device(volume, ray_weights, shear_weights, shear_offsets, measured):
    rows, cols = lax.axis_size("row"), lax.axis_size("col")
    slices, slab_rows, width = volume.shape
    angles = ray_weights.shape[0]
    owned = measured.shape[0]
    count = rows * cols
    homes = Homes(rows, cols, angles)
    per = homes.per
    f32, bf16 = jnp.float32, jnp.bfloat16
    dma = pltpu.SemaphoreType.DMA
    vmem = pl.BlockSpec(memory_space=pltpu.VMEM)
    hbm = pl.BlockSpec(memory_space=pltpu.HBM)

    def blocks(*number):
        return pltpu.VMEM((*number, slices, width), f32)

    columns, spread, resid = pl.pallas_call(
        functools.partial(exchange, rows, cols, 1.0 / math.sqrt(slab_rows * rows), homes),
        out_shape=(
            jax.ShapeDtypeStruct((slab_rows, 3 * angles), bf16),
            jax.ShapeDtypeStruct((slices, 3 * angles, width), bf16),
            jax.ShapeDtypeStruct(measured.shape, f32)),
        in_specs=[hbm] * 5,
        out_specs=(vmem, vmem, vmem),
        scratch_shapes=[
            pltpu.VMEM(volume.shape, f32),
            pltpu.VMEM(ray_weights.shape, f32),
            pltpu.VMEM((per, width, width), shear_weights.dtype),
            pltpu.SMEM(shear_offsets.shape, jnp.int32),
            blocks(owned),
            pltpu.VMEM((angles * slices, width), f32),
            pltpu.VMEM((count, per * slices, width), f32),
            blocks(cols, per), blocks(cols, per), blocks(per, cols), blocks(count, per), blocks(angles), blocks(owned),
            dma((slices,)), dma((4,)), dma, dma, dma, dma, dma, dma, dma, dma,
        ],
        compiler_params=pltpu.CompilerParams(collective_id=0, has_side_effects=True, vmem_limit_bytes=KERNEL_VMEM),
        name="exchange",
    )(*(pltpu.with_memory_space_constraint(value, pltpu.HBM)
        for value in (volume, ray_weights, shear_weights, shear_offsets, measured)))
    return pl.pallas_call(
        finish,
        out_shape=(jax.ShapeDtypeStruct(measured.shape, f32), jax.ShapeDtypeStruct(volume.shape, f32)),
        in_specs=[vmem] * 3,
        out_specs=(hbm, hbm),
        scratch_shapes=[pltpu.VMEM(volume.shape, f32), dma((slices,)), dma],
        compiler_params=pltpu.CompilerParams(vmem_limit_bytes=KERNEL_VMEM),
        name="finish",
    )(columns, spread, resid)


def solution(mesh):
    placed = (P(None, "row", "col"), P(None, "row"), P(), P(), P("row", None, "col"))
    return jax.shard_map(
        on_device,
        mesh=mesh,
        in_specs=placed,
        out_specs=(P("row", None, "col"), P(None, "row", "col")),
        check_vma=False,
    )
```

time: 17.5 us -> 16.3 us (0.931)
  Pallas kernels: 16.8 us -> 15.6 us
    pallas_call x1, Pallas kernels: 15.6 us -> 14.3 us  [on_device(): pl.pallas_call(functools.partial(exchange, rows, cols, 1.0 / math.sqrt(sl...]
where the time goes in v1:
time: 16.3 us; the launch traced here: 16.2 us
  Pallas kernels  15.6 us (96%)
  between operations  0.64 us (4%)
    pallas_call x1, Pallas kernels, on_device(): pl.pallas_call(functools.partial(exchange, rows, cols, 1.0 / math.sqrt(sl...  14.3 us
    pallas_call x1, Pallas kernels, on_device(): pl.pallas_call(finish, out_shape=(jax.ShapeDtypeStruct(measured.shape, f3...  1.2 us

profile of v1, /device:TPU:0, one launch (start us, length us, event | category | flops | bytes accessed | tf_op | source)
XLA Modules:
  0.0 16.2 jit_solution(9464902205925081702)
XLA Ops:
  0.6 14.3 %exchange.1 = (bf16[256,48]{1,0:T(8,128)(2,1)S(1)}, bf16[8,48,128]{2,1,0:T(8,128)(2,1)S(1)}, f32[4,8,128]{2,1,0:T(8,128)S(1)}) custom-call(f32[8,256,128]{2,1,0:T(8,128)} %volume_ref.1, f32[16,256]{1,0:T(8,128)} %weights_ref.1, bf16[16,128,128]{2,1,0:T(8,128)(2,1)} %shear_ref.1, s32[16]{0:T(128)} %offsets_ref.1, f32[4,8,128]{2,1,0:T(8,128)} %measured_ref.1), custom_call_target="tpu_custom_call" | custom-call | tf_op jit(solution)/shard_map/exchange/pallas_call | solution.py:300
  15.0 1.2 %finish.1 = (f32[4,8,128]{2,1,0:T(8,128)}, f32[8,256,128]{2,1,0:T(8,128)}) custom-call(bf16[256,48]{1,0:T(8,128)(2,1)S(1)} %get-tuple-element.5.columns_ref, bf16[8,48,128]{2,1,0:T(8,128)(2,1)S(1)} %get-tuple-element.6.spread_ref, f32[4,8,128]{2,1,0:T(8,128)S(1)} %get-tuple-element.7.resid_ref), custom_call_target="tpu_custom_call" | custom-call | tf_op jit(solution)/shard_map/finish/pallas_call | solution.py:323

commit v2 on v1

v2 whole, which is shorter than its diff:
```python
import functools
import math

import jax
import jax.numpy as jnp
from jax import lax
from jax.experimental import pallas as pl
from jax.experimental.pallas import tpu as pltpu
from jax.sharding import PartitionSpec as P

MESH = pl.DeviceIdType.MESH
UNROLL_UP_TO = 64
KERNEL_VMEM = 24 * 1024 * 1024
LATE_COLUMNS = 8
CHUNK = 2
GROUP = 4


def split(value):
    high = value.astype(jnp.bfloat16)
    return high, (value - high.astype(jnp.float32)).astype(jnp.bfloat16)


def each(count, body):
    if count <= UNROLL_UP_TO:
        for step in range(count):
            body(step)
    else:
        lax.fori_loop(0, count, lambda step, _: (body(step), 0)[1], 0)


def bytes_of(ref, blocks, sem):
    part = ref.at[pl.ds(0, blocks)]
    return pltpu.make_async_copy(part, part, sem)


class Homes:
    def __init__(self, rows, cols, angles):
        self.owned = angles // rows
        self.per = 2 if self.owned % 2 == 0 else 1
        self.count = angles // self.per
        pair = 2 if rows % 2 == 0 and self.count < rows * cols // 2 else 1

        def far(place):
            group, half, deep = place[0] // pair, place[1] % 2, place[1] // 2
            return 10 * group + 10 * half + 11 * deep + 15 * group * half

        devices = [(row, col) for row in range(pair - 1, rows, pair) for col in range(cols)]
        devices.sort(key=lambda place: (far(place), place))
        skipped = 1 if self.count < len(devices) else 0
        self.places = sorted(devices[skipped:skipped + self.count])
        self.order = sorted(range(self.count), key=lambda home: (self.places[home][1] // 2, home))

    def owner(self, home):
        return home * self.per // self.owned


def wrap(index, size):
    return lax.rem(index, size) if size & (size - 1) else jnp.bitwise_and(index, size - 1)


def pick(later, first, second):
    return tuple(lax.select(later, jnp.int32(after), jnp.int32(before)) for before, after in zip(first, second))


def exchange(
    rows, cols, factor, homes,
    volume_ref, weights_ref, shear_ref, offsets_ref, measured_ref,
    columns_ref, pulled, resid_in,
    slab, weights_in, shear, turned, offsets, measured, tiles, landed, measure_in, resid, spreads, pulls,
    slab_sem, local_sem, out_sem, in_sem, back_out_sem, back_in_sem, m_out_sem, m_in_sem, r_out_sem, r_in_sem,
):
    slices = volume_ref.shape[0]
    angles = weights_ref.shape[0]
    owned = measured_ref.shape[0]
    width = volume_ref.shape[2]
    per = homes.per
    own_homes = owned // per
    count = rows * cols
    row, col = lax.axis_index("row"), lax.axis_index("col")
    me = row * cols + col
    hits = [me == place[0] * cols + place[1] for place in homes.places]
    at_home = functools.reduce(jnp.logical_or, hits)
    away = jnp.logical_not(at_home)
    mine = sum(hit.astype(jnp.int32) * home for home, hit in enumerate(hits))
    owner = homes.owner(mine)
    owner_here = jnp.logical_and(at_home, owner == row)
    owner_there = jnp.logical_and(at_home, owner != row)
    late = col >= cols - cols // LATE_COLUMNS

    def others(body, start=0, stop=count - 1, last_first=False):
        rank = col * rows + row

        def at(step):
            step = count - 2 - step if last_first else step
            index = step + (step >= rank).astype(jnp.int32)
            body(lax.rem(index, rows) * cols + index // rows, (lax.rem(index, rows), index // rows))

        if count <= UNROLL_UP_TO:
            for step in range(start, stop):
                at(step)
        else:
            lax.fori_loop(start, stop, lambda step, carry: (at(step), carry)[1], 0)

    def send(source, target, send_sem, recv_sem, place):
        pltpu.make_async_remote_copy(
            src_ref=source, dst_ref=target, send_sem=send_sem, recv_sem=recv_sem,
            device_id=place, device_id_type=MESH).start()

    block = per * slices
    barrier = pltpu.get_barrier_semaphore()

    weights_copy = pltpu.make_async_copy(weights_ref, weights_in, local_sem.at[0])
    weights_copy.start()
    measured_copy = pltpu.make_async_copy(measured_ref, measured, local_sem.at[2])
    measured_copy.start()
    volume_copies = []
    for s in range(0, slices, CHUNK):
        copy = pltpu.make_async_copy(volume_ref.at[pl.ds(s, CHUNK)], slab.at[pl.ds(s, CHUNK)], slab_sem.at[s])
        copy.start()
        volume_copies.append(copy)

    @pl.when(at_home)
    def _():
        others(lambda index, place: pl.semaphore_signal(barrier, inc=1, device_id=place, device_id_type=MESH),
               last_first=True)

    shear_copy = pltpu.make_async_copy(shear_ref.at[pl.ds(mine * per, per)], shear, local_sem.at[1])
    shear_copy.start()
    offsets_copy = pltpu.make_async_copy(offsets_ref, offsets, local_sem.at[3])
    offsets_copy.start()

    def meet():
        @pl.when(at_home)
        def _():
            pl.semaphore_wait(barrier, homes.count - 1)

        @pl.when(away)
        def _():
            pl.semaphore_wait(barrier, homes.count)

    def send_measured():
        measured_copy.wait()
        for r in range(rows):
            @pl.when(row == r)
            def _():
                for k in range(own_homes):
                    place = homes.places[r * own_homes + k]
                    if place[0] != r:
                        send(measured.at[pl.ds(k * per, per)], measure_in.at[col], m_out_sem, m_in_sem, place)
                        continue

                    @pl.when(col != place[1])
                    def _():
                        send(measured.at[pl.ds(k * per, per)], measure_in.at[col], m_out_sem, m_in_sem, place)

                    @pl.when(col == place[1])
                    def _():
                        measure_in[col] = measured[k * per:(k + 1) * per]

    @pl.when(late)
    def _():
        meet()
        send_measured()

    weights_copy.wait()
    weights = weights_in[...] * factor
    w_high, w_low = split(weights)
    w_both = jnp.concatenate([w_high, w_low], axis=0)
    for s in range(0, slices, GROUP):
        for copy in volume_copies[s // CHUNK:(s + GROUP) // CHUNK]:
            copy.wait()
        v_high, v_low = split(jnp.concatenate([slab[s + i] for i in range(GROUP)], axis=1))
        first = jnp.dot(w_both, v_high, preferred_element_type=jnp.float32)
        second = jnp.dot(w_high, v_low, preferred_element_type=jnp.float32)
        total = first[:angles] + first[angles:] + second
        for i in range(GROUP):
            tiles[pl.ds(s + i, angles, stride=slices), :] = total[:, i * width:(i + 1) * width]

    pl.when(jnp.logical_not(late))(meet)

    order = homes.order
    rank = sum((mine == home).astype(jnp.int32) * turn for turn, home in enumerate(order))
    rank = lax.select(at_home, rank, jnp.int32(homes.count))

    def send_tile(turn):
        before, after = order[turn], order[min(turn + 1, homes.count - 1)]
        home, *place = pick(turn >= rank, (before, *homes.places[before]), (after, *homes.places[after]))
        source = tiles.at[pl.ds(pl.multiple_of(home * block, block), block)]
        send(source, landed.at[me], out_sem, in_sem, tuple(place))

    for turn in range(homes.count - 1):
        send_tile(turn)
    pl.when(away)(functools.partial(send_tile, homes.count - 1))
    pl.when(jnp.logical_not(late))(send_measured)
    shear_copy.wait()
    offsets_copy.wait()

    columns_ref[...] = jnp.concatenate(
        [weights, weights - w_high.astype(jnp.float32), weights], axis=0).T.astype(jnp.bfloat16)

    @pl.when(at_home)
    def _():
        landed[me] = tiles[pl.ds(pl.multiple_of(mine * block, block), block), :]
        for slot in range(per):
            turned[slot] = shear[slot].T

    @pl.when(owner_here)
    def _():
        bytes_of(measured, owned - per, m_out_sem).wait()

    @pl.when(jnp.logical_not(owner_here))
    def _():
        bytes_of(measured, owned, m_out_sem).wait()

    @pl.when(owner_here)
    def _():
        bytes_of(measure_in, cols - 1, m_in_sem).wait()

    @pl.when(owner_there)
    def _():
        bytes_of(measure_in, cols, m_in_sem).wait()

    @pl.when(at_home)
    def _():
        first = lax.rem(mine, own_homes) * per
        owned_here = owner == row

        def send_pull(index, place):
            send(pulls.at[index], pulled.at[pl.ds(mine * per, per)], back_out_sem, back_in_sem, place)

        def send_resid(step):
            c = wrap(col + step, cols)
            send(resid.at[c], resid_in.at[pl.ds(first, per)], r_out_sem, r_in_sem, (owner, c))

        shifts = [[wrap(offsets[mine * per + slot] * r, cols) for r in range(rows)] for slot in range(per)]
        bytes_of(landed, count - 1, in_sem).wait()
        lines = []
        for slot in range(per):
            part = slice(slot * slices, (slot + 1) * slices)
            totals = []
            for c in range(cols):
                total = landed[c, part]
                for r in range(1, rows):
                    total = total + landed[r * cols + wrap(cols - shifts[slot][r] + c, cols), part]
                totals.append(total)
            both = jnp.concatenate(split(jnp.concatenate(totals, axis=0)), axis=1)
            twice = jnp.concatenate([shear[slot]] * 2, axis=0)
            line = jnp.dot(both, twice, preferred_element_type=jnp.float32)
            line = line - jnp.concatenate([measure_in[c, slot] for c in range(cols)], axis=0)
            for c in range(cols):
                resid[c, slot] = line[c * slices:(c + 1) * slices]
            lines.append(line)
        for slot in range(per):
            both = jnp.concatenate(split(lines[slot]), axis=1)
            twice = jnp.concatenate([turned[slot]] * 2, axis=0)
            spread = jnp.dot(both, twice, preferred_element_type=jnp.float32)
            for c in range(cols):
                spreads[slot, c] = spread[c * slices:(c + 1) * slices]
            for r in range(rows):
                for c in range(cols):
                    pulls[r * cols + c, slot] = spreads[slot, wrap(shifts[slot][r] + c, cols)]
        others(send_pull, stop=rows)
        each(cols - 1, lambda step: send_resid(step + 1))
        pl.when(jnp.logical_not(owned_here))(functools.partial(send_resid, 0))
        others(send_pull, start=rows)
        pulled[pl.ds(mine * per, per)] = pulls[me]

        @pl.when(owned_here)
        def _():
            resid_in[pl.ds(first, per)] = resid[col]

        bytes_of(tiles, (homes.count - 1) * block, out_sem).wait()
        bytes_of(pulled, angles - per, back_in_sem).wait()

    @pl.when(away)
    def _():
        bytes_of(tiles, homes.count * block, out_sem).wait()
        bytes_of(pulled, angles, back_in_sem).wait()

    @pl.when(owner_here)
    def _():
        bytes_of(resid_in, owned - per, r_in_sem).wait()
        bytes_of(resid, cols - 1, r_out_sem).wait()

    @pl.when(jnp.logical_not(owner_here))
    def _():
        bytes_of(resid_in, owned, r_in_sem).wait()

    @pl.when(owner_there)
    def _():
        bytes_of(resid, cols, r_out_sem).wait()

    @pl.when(at_home)
    def _():
        bytes_of(pulls, count - 1, back_out_sem).wait()


def finish(columns_ref, pulled_ref, resid_ref, residual_ref, gradient_ref, stage, stage_sem, resid_sem):
    copies = [pltpu.make_async_copy(resid_ref, residual_ref, resid_sem)]
    copies[0].start()
    for s in range(pulled_ref.shape[1]):
        high, low = split(pulled_ref[:, s, :])
        spread = jnp.concatenate([high, high, low], axis=0)
        stage[s] = jnp.dot(columns_ref[...], spread, preferred_element_type=jnp.float32)
        copy = pltpu.make_async_copy(stage.at[s], gradient_ref.at[s], stage_sem.at[s])
        copy.start()
        copies.append(copy)
    for copy in copies:
        copy.wait()


def on_device(volume, ray_weights, shear_weights, shear_offsets, measured):
    rows, cols = lax.axis_size("row"), lax.axis_size("col")
    slices, slab_rows, width = volume.shape
    angles = ray_weights.shape[0]
    owned = measured.shape[0]
    count = rows * cols
    homes = Homes(rows, cols, angles)
    per = homes.per
    f32, bf16 = jnp.float32, jnp.bfloat16
    dma = pltpu.SemaphoreType.DMA
    vmem = pl.BlockSpec(memory_space=pltpu.VMEM)
    hbm = pl.BlockSpec(memory_space=pltpu.HBM)

    def blocks(*number):
        return pltpu.VMEM((*number, slices, width), f32)

    columns, pulled, resid = pl.pallas_call(
        functools.partial(exchange, rows, cols, 1.0 / math.sqrt(slab_rows * rows), homes),
        out_shape=(
            jax.ShapeDtypeStruct((slab_rows, 3 * angles), bf16),
            jax.ShapeDtypeStruct((angles, slices, width), f32),
            jax.ShapeDtypeStruct(measured.shape, f32)),
        in_specs=[hbm] * 5,
        out_specs=(vmem, vmem, vmem),
        scratch_shapes=[
            pltpu.VMEM(volume.shape, f32),
            pltpu.VMEM(ray_weights.shape, f32),
            pltpu.VMEM((per, width, width), shear_weights.dtype),
            pltpu.VMEM((per, width, width), shear_weights.dtype),
            pltpu.SMEM(shear_offsets.shape, jnp.int32),
            blocks(owned),
            pltpu.VMEM((angles * slices, width), f32),
            pltpu.VMEM((count, per * slices, width), f32),
            blocks(cols, per), blocks(cols, per), blocks(per, cols), blocks(count, per),
            dma((slices,)), dma((4,)), dma, dma, dma, dma, dma, dma, dma, dma,
        ],
        compiler_params=pltpu.CompilerParams(collective_id=0, has_side_effects=True, vmem_limit_bytes=KERNEL_VMEM),
        name="exchange",
    )(*(pltpu.with_memory_space_constraint(value, pltpu.HBM)
        for value in (volume, ray_weights, shear_weights, shear_offsets, measured)))
    return pl.pallas_call(
        finish,
        out_shape=(jax.ShapeDtypeStruct(measured.shape, f32), jax.ShapeDtypeStruct(volume.shape, f32)),
        in_specs=[vmem] * 3,
        out_specs=(hbm, hbm),
        scratch_shapes=[pltpu.VMEM(volume.shape, f32), dma((slices,)), dma],
        compiler_params=pltpu.CompilerParams(vmem_limit_bytes=KERNEL_VMEM),
        name="finish",
    )(columns, pulled, resid)


def solution(mesh):
    placed = (P(None, "row", "col"), P(None, "row"), P(), P(), P("row", None, "col"))
    return jax.shard_map(
        on_device,
        mesh=mesh,
        in_specs=placed,
        out_specs=(P("row", None, "col"), P(None, "row", "col")),
        check_vma=False,
    )
```

time: 16.3 us -> 15.1 us (0.926)
  Pallas kernels: 15.6 us -> 14.3 us
    pallas_call x1, Pallas kernels: 14.3 us -> 13.1 us  [on_device(): pl.pallas_call(functools.partial(exchange, rows, cols, 1.0 / math.sqrt(sl...]
where the time goes in v2:
time: 15.1 us; the launch traced here: 15 us
  Pallas kernels  14.3 us (95%)
  between operations  0.64 us (4%)
    pallas_call x1, Pallas kernels, on_device(): pl.pallas_call(functools.partial(exchange, rows, cols, 1.0 / math.sqrt(sl...  13.1 us
    pallas_call x1, Pallas kernels, on_device(): pl.pallas_call(finish, out_shape=(jax.ShapeDtypeStruct(measured.shape, f3...  1.24 us

profile of v2, /device:TPU:0, one launch (start us, length us, event | category | flops | bytes accessed | tf_op | source)
XLA Modules:
  0.0 15.0 jit_solution(2813503598095883959)
XLA Ops:
  0.6 13.1 %exchange.1 = (bf16[256,48]{1,0:T(8,128)(2,1)S(1)}, f32[16,8,128]{2,1,0:T(8,128)S(1)}, f32[4,8,128]{2,1,0:T(8,128)S(1)}) custom-call(f32[8,256,128]{2,1,0:T(8,128)} %volume_ref.1, f32[16,256]{1,0:T(8,128)} %weights_ref.1, bf16[16,128,128]{2,1,0:T(8,128)(2,1)} %shear_ref.1, s32[16]{0:T(128)} %offsets_ref.1, f32[4,8,128]{2,1,0:T(8,128)} %measured_ref.1), custom_call_target="tpu_custom_call" | custom-call | tf_op jit(solution)/shard_map/exchange/pallas_call | solution.py:329
  13.7 1.2 %finish.1 = (f32[4,8,128]{2,1,0:T(8,128)}, f32[8,256,128]{2,1,0:T(8,128)}) custom-call(bf16[256,48]{1,0:T(8,128)(2,1)S(1)} %get-tuple-element.5.columns_ref, f32[16,8,128]{2,1,0:T(8,128)S(1)} %get-tuple-element.6.pulled_ref, f32[4,8,128]{2,1,0:T(8,128)S(1)} %get-tuple-element.7.resid_ref), custom_call_target="tpu_custom_call" | custom-call | tf_op jit(solution)/shard_map/finish/pallas_call | solution.py:353

commit v3 on v2

v3 whole, which is shorter than its diff:
```python
import functools
import math

import jax
import jax.numpy as jnp
from jax import lax
from jax.experimental import pallas as pl
from jax.experimental.pallas import tpu as pltpu
from jax.sharding import PartitionSpec as P

MESH = pl.DeviceIdType.MESH
UNROLL_UP_TO = 64
KERNEL_VMEM = 24 * 1024 * 1024
LATE_COLUMNS = 4
HALVES = 2


def split(value):
    high = value.astype(jnp.bfloat16)
    return high, (value - high.astype(jnp.float32)).astype(jnp.bfloat16)


def each(count, body):
    if count <= UNROLL_UP_TO:
        for step in range(count):
            body(step)
    else:
        lax.fori_loop(0, count, lambda step, _: (body(step), 0)[1], 0)


def bytes_of(ref, blocks, sem):
    part = ref.at[pl.ds(0, blocks)]
    return pltpu.make_async_copy(part, part, sem)


class Homes:
    def __init__(self, rows, cols, angles):
        self.owned = angles // rows
        self.per = 2 if self.owned % 2 == 0 else 1
        self.count = angles // self.per
        pair = 2 if rows % 2 == 0 and self.count < rows * cols // 2 else 1

        def far(place):
            group, half, deep = place[0] // pair, place[1] % 2, place[1] // 2
            return 10 * group + 10 * half + 11 * deep + 15 * group * half

        devices = [(row, col) for row in range(pair - 1, rows, pair) for col in range(cols)]
        devices.sort(key=lambda place: (far(place), place))
        skipped = 1 if self.count < len(devices) else 0
        self.places = sorted(devices[skipped:skipped + self.count])
        self.order = sorted(range(self.count), key=lambda home: (self.places[home][1] // 2, home))

    def owner(self, home):
        return home * self.per // self.owned


def wrap(index, size):
    return lax.rem(index, size) if size & (size - 1) else jnp.bitwise_and(index, size - 1)


def pick(later, first, second):
    return tuple(lax.select(later, jnp.int32(after), jnp.int32(before)) for before, after in zip(first, second))


def exchange(
    rows, cols, factor, homes,
    volume_ref, weights_ref, shear_ref, offsets_ref, measured_ref,
    columns_ref, pulled, resid_in,
    slab, weights_in, shear, gains, offsets, measured, leaving, tiles, landed, measure_in, resid, spreads, pulls,
    slab_sem, local_sem, out_sem, in_sem, back_in_sem, m_out_sem, m_in_sem, r_in_sem,
):
    slices = volume_ref.shape[0]
    angles = weights_ref.shape[0]
    owned = measured_ref.shape[0]
    width = volume_ref.shape[2]
    per = homes.per
    own_homes = owned // per
    count = rows * cols
    row, col = lax.axis_index("row"), lax.axis_index("col")
    me = row * cols + col
    hits = [me == place[0] * cols + place[1] for place in homes.places]
    at_home = functools.reduce(jnp.logical_or, hits)
    away = jnp.logical_not(at_home)
    mine = sum(hit.astype(jnp.int32) * home for home, hit in enumerate(hits))
    owner = homes.owner(mine)
    owner_here = jnp.logical_and(at_home, owner == row)
    owner_there = jnp.logical_and(at_home, owner != row)
    late = col >= cols - cols // LATE_COLUMNS

    def others(body, start=0, stop=count - 1, last_first=False):
        rank = col * rows + row

        def at(step):
            step = count - 2 - step if last_first else step
            index = step + (step >= rank).astype(jnp.int32)
            body(lax.rem(index, rows) * cols + index // rows, (lax.rem(index, rows), index // rows))

        if count <= UNROLL_UP_TO:
            for step in range(start, stop):
                at(step)
        else:
            lax.fori_loop(start, stop, lambda step, carry: (at(step), carry)[1], 0)

    def send(source, target, send_sem, recv_sem, place):
        pltpu.make_async_remote_copy(
            src_ref=source, dst_ref=target, send_sem=send_sem, recv_sem=recv_sem,
            device_id=place, device_id_type=MESH).start()

    group = slices // HALVES
    block = per * group
    barrier = pltpu.get_barrier_semaphore()

    weights_copy = pltpu.make_async_copy(weights_ref, weights_in, local_sem.at[0])
    weights_copy.start()
    measured_copy = pltpu.make_async_copy(measured_ref, measured, local_sem.at[1])
    measured_copy.start()
    volume_copies = []
    for half in range(HALVES):
        part = pl.ds(half * group, group)
        copy = pltpu.make_async_copy(volume_ref.at[part], slab.at[part], slab_sem.at[half])
        copy.start()
        volume_copies.append(copy)

    @pl.when(at_home)
    def _():
        others(lambda index, place: pl.semaphore_signal(barrier, inc=1, device_id=place, device_id_type=MESH),
               last_first=True)

    def meet():
        @pl.when(at_home)
        def _():
            pl.semaphore_wait(barrier, homes.count - 1)

        @pl.when(away)
        def _():
            pl.semaphore_wait(barrier, homes.count)

    def send_measured():
        measured_copy.wait()
        for s in range(slices):
            leaving[s // group, pl.ds(s % group, owned, stride=group), :] = measured[:, s, :]
        for r in range(rows):
            @pl.when(row == r)
            def _():
                for k in range(own_homes):
                    place = homes.places[r * own_homes + k]
                    source = leaving.at[:, pl.ds(k * block, block)]
                    if place[0] != r:
                        send(source, measure_in.at[col], m_out_sem, m_in_sem, place)
                        continue

                    @pl.when(col != place[1])
                    def _():
                        send(source, measure_in.at[col], m_out_sem, m_in_sem, place)

                    @pl.when(col == place[1])
                    def _():
                        measure_in[col] = leaving[:, k * block:(k + 1) * block]

    @pl.when(late)
    def _():
        meet()
        send_measured()

    weights_copy.wait()
    weights = weights_in[...] * factor
    w_high, w_low = split(weights)
    w_both = jnp.concatenate([w_high, w_low], axis=0)
    def send_tiles(halves):
        order = homes.order
        rank = sum((mine == home).astype(jnp.int32) * turn for turn, home in enumerate(order))
        rank = lax.select(at_home, rank, jnp.int32(homes.count))

        def send_tile(half, turn):
            before, after = order[turn], order[min(turn + 1, homes.count - 1)]
            home, *place = pick(turn >= rank, (before, *homes.places[before]), (after, *homes.places[after]))
            source = tiles.at[half, pl.ds(pl.multiple_of(home * block, block), block)]
            send(source, landed.at[me, half], out_sem, in_sem, tuple(place))

        for half in halves:
            for turn in range(homes.count - 1):
                send_tile(half, turn)

        @pl.when(away)
        def _():
            for half in halves:
                send_tile(half, homes.count - 1)

    for half in range(HALVES):
        volume_copies[half].wait()
        v_high, v_low = split(jnp.concatenate([slab[half * group + i] for i in range(group)], axis=1))
        first = jnp.dot(w_both, v_high, preferred_element_type=jnp.float32)
        second = jnp.dot(w_high, v_low, preferred_element_type=jnp.float32)
        total = first[:angles] + first[angles:] + second
        for i in range(group):
            tiles[half, pl.ds(i, angles, stride=group), :] = total[:, i * width:(i + 1) * width]
        if half < HALVES - 1:
            pl.when(late)(functools.partial(send_tiles, [half]))

    @pl.when(late)
    def _():
        send_tiles([HALVES - 1])

    @pl.when(jnp.logical_not(late))
    def _():
        meet()
        send_tiles(range(HALVES))

    pl.when(jnp.logical_not(late))(send_measured)
    shear_copy = pltpu.make_async_copy(shear_ref.at[pl.ds(mine * per, per)], shear, local_sem.at[0])
    shear_copy.start()
    offsets_copy = pltpu.make_async_copy(offsets_ref, offsets, local_sem.at[1])
    offsets_copy.start()

    columns_ref[...] = jnp.concatenate(
        [weights, weights - w_high.astype(jnp.float32), weights], axis=0).T.astype(jnp.bfloat16)

    @pl.when(at_home)
    def _():
        landed[me] = tiles[:, pl.ds(pl.multiple_of(mine * block, block), block), :]
    shear_copy.wait()
    offsets_copy.wait()

    @pl.when(at_home)
    def _():
        for slot in range(per):
            part = slice(slot * width, (slot + 1) * width)
            square = lax.dot_general(
                shear[slot], shear[slot], (((1,), (1,)), ((), ())), preferred_element_type=jnp.float32)
            gains[0, :, part], gains[1, :, part] = split(square)
            gains[2, :, part] = shear[slot]
            gains[3, :, part] = shear[slot].T

    @pl.when(at_home)
    def _():
        bytes_of(pulls, homes.count - 1, out_sem).wait()

    @pl.when(away)
    def _():
        bytes_of(pulls, homes.count, out_sem).wait()

    @pl.when(owner_here)
    def _():
        bytes_of(measure_in, own_homes - 1, m_out_sem).wait()

    @pl.when(jnp.logical_not(owner_here))
    def _():
        bytes_of(measure_in, own_homes, m_out_sem).wait()

    @pl.when(owner_here)
    def _():
        bytes_of(measure_in, cols - 1, m_in_sem).wait()

    @pl.when(owner_there)
    def _():
        bytes_of(measure_in, cols, m_in_sem).wait()

    @pl.when(at_home)
    def _():
        first = pl.ds(pl.multiple_of(lax.rem(mine, own_homes) * block, block), block)
        here = pl.ds(pl.multiple_of(mine * block, block), block)
        owned_here = owner == row

        def send_pull(index, place):
            send(pulls.at[index], pulled.at[:, here], out_sem, back_in_sem, place)

        def send_resid(step):
            c = step + (step >= lax.select(owned_here, col, jnp.int32(cols))).astype(jnp.int32)
            send(resid.at[c], resid_in.at[:, first], m_out_sem, r_in_sem, (owner, c))

        def by_slot(parts):
            chosen = parts[0]
            for slot in range(1, per):
                chosen = jnp.where(slot_of[:chosen.shape[0]] >= slot, parts[slot], chosen)
            return chosen

        def times(high, low, right, rest=None):
            product = jnp.dot(jnp.concatenate([high, low], axis=1), jnp.concatenate([right] * 2, axis=0),
                              preferred_element_type=jnp.float32)
            if rest is not None:
                product = product + jnp.dot(high, rest, preferred_element_type=jnp.float32)
            return by_slot([product[:, slot * width:(slot + 1) * width] for slot in range(per)])

        height = HALVES * cols * block
        slot_of = lax.rem(lax.broadcasted_iota(jnp.int32, (height, width), 0), block) // group
        shifts = [[wrap(offsets[mine * per + slot] * r, cols) for r in range(rows)] for slot in range(per)]
        bytes_of(landed, count - 1, in_sem).wait()
        totals = []
        for c in range(cols):
            sources = [[wrap(cols - shifts[slot][r] + c, cols) for slot in range(per)] for r in range(rows)]
            for half in range(HALVES):
                total = landed[c, half]
                for r in range(1, rows):
                    total = total + by_slot([landed[r * cols + sources[r][slot], half] for slot in range(per)])
                totals.append(total)
        t_high, t_low = split(jnp.concatenate(totals, axis=0))
        level = jnp.concatenate([measure_in[c, half] for c in range(cols) for half in range(HALVES)], axis=0)
        spread = times(t_high, t_low, gains[0], gains[1]) - times(*split(level), gains[3])
        line = times(t_high, t_low, gains[2]) - level
        for c in range(cols):
            for half in range(HALVES):
                at = (c * HALVES + half) * block
                resid[c, half] = line[at:at + block]
        for c in range(cols):
            for half in range(HALVES):
                at = (c * HALVES + half) * block
                spreads[c, half] = spread[at:at + block]
        for c in range(cols):
            for half in range(HALVES):
                pulls[c, half] = spreads[c, half]
        for r in range(1, rows):
            for c in range(cols):
                sources = [wrap(shifts[slot][r] + c, cols) for slot in range(per)]
                for half in range(HALVES):
                    pulls[r * cols + c, half] = by_slot([spreads[source, half] for source in sources])
        others(send_pull, stop=2)
        send_resid(0)
        others(send_pull, start=2, stop=3 * rows)
        each(cols - 2, lambda step: send_resid(step + 1))
        pl.when(jnp.logical_not(owned_here))(functools.partial(send_resid, cols - 1))
        others(send_pull, start=3 * rows)
        pulled[:, here] = pulls[me]

        @pl.when(owned_here)
        def _():
            resid_in[:, first] = resid[col]

        bytes_of(pulls, homes.count - 1, back_in_sem).wait()

    @pl.when(away)
    def _():
        bytes_of(pulls, homes.count, back_in_sem).wait()

    @pl.when(owner_here)
    def _():
        bytes_of(resid, own_homes - 1, r_in_sem).wait()
        bytes_of(resid, cols - 1, m_out_sem).wait()

    @pl.when(jnp.logical_not(owner_here))
    def _():
        bytes_of(resid, own_homes, r_in_sem).wait()

    @pl.when(owner_there)
    def _():
        bytes_of(resid, cols, m_out_sem).wait()

    @pl.when(at_home)
    def _():
        bytes_of(pulls, count - 1, out_sem).wait()


def finish(columns_ref, pulled_ref, resid_ref, residual_ref, gradient_ref, stage, natural, stage_sem, resid_sem):
    owned, slices, width = natural.shape
    group = slices // HALVES
    angles = pulled_ref.shape[1] // group
    for s in range(slices):
        high, low = split(pulled_ref[s // group, pl.ds(s % group, angles, stride=group), :])
        spread = jnp.concatenate([high, high, low], axis=0)
        stage[s] = jnp.dot(columns_ref[...], spread, preferred_element_type=jnp.float32)
        pltpu.make_async_copy(stage.at[s], gradient_ref.at[s], stage_sem).start()
        natural[:, s, :] = resid_ref[s // group, pl.ds(s % group, owned, stride=group), :]
    copy = pltpu.make_async_copy(natural, residual_ref, resid_sem)
    copy.start()
    pltpu.make_async_copy(stage, gradient_ref, stage_sem).wait()
    copy.wait()


def on_device(volume, ray_weights, shear_weights, shear_offsets, measured):
    rows, cols = lax.axis_size("row"), lax.axis_size("col")
    slices, slab_rows, width = volume.shape
    angles = ray_weights.shape[0]
    owned = measured.shape[0]
    count = rows * cols
    homes = Homes(rows, cols, angles)
    per = homes.per
    f32, bf16 = jnp.float32, jnp.bfloat16
    dma = pltpu.SemaphoreType.DMA
    vmem = pl.BlockSpec(memory_space=pltpu.VMEM)
    hbm = pl.BlockSpec(memory_space=pltpu.HBM)

    group = slices // HALVES

    def halves(*number):
        return pltpu.VMEM((*number, HALVES, per * group, width), f32)

    columns, pulled, resid = pl.pallas_call(
        functools.partial(exchange, rows, cols, 1.0 / math.sqrt(slab_rows * rows), homes),
        out_shape=(
            jax.ShapeDtypeStruct((slab_rows, 3 * angles), bf16),
            jax.ShapeDtypeStruct((HALVES, angles * group, width), f32),
            jax.ShapeDtypeStruct((HALVES, owned * group, width), f32)),
        in_specs=[hbm] * 5,
        out_specs=(vmem, vmem, vmem),
        scratch_shapes=[
            pltpu.VMEM(volume.shape, f32),
            pltpu.VMEM(ray_weights.shape, f32),
            pltpu.VMEM((per, width, width), shear_weights.dtype),
            pltpu.VMEM((4, width, per * width), shear_weights.dtype),
            pltpu.SMEM(shear_offsets.shape, jnp.int32),
            pltpu.VMEM(measured.shape, f32),
            pltpu.VMEM((HALVES, owned * group, width), f32),
            pltpu.VMEM((HALVES, angles * group, width), f32),
            halves(count), halves(cols), halves(cols), halves(cols), halves(count),
            dma((HALVES,)), dma((2,)), dma, dma, dma, dma, dma, dma,
        ],
        compiler_params=pltpu.CompilerParams(collective_id=0, has_side_effects=True, vmem_limit_bytes=KERNEL_VMEM),
        name="exchange",
    )(*(pltpu.with_memory_space_constraint(value, pltpu.HBM)
        for value in (volume, ray_weights, shear_weights, shear_offsets, measured)))
    return pl.pallas_call(
        finish,
        out_shape=(jax.ShapeDtypeStruct(measured.shape, f32), jax.ShapeDtypeStruct(volume.shape, f32)),
        in_specs=[vmem] * 3,
        out_specs=(hbm, hbm),
        scratch_shapes=[pltpu.VMEM(volume.shape, f32), pltpu.VMEM(measured.shape, f32), dma, dma],
        compiler_params=pltpu.CompilerParams(vmem_limit_bytes=KERNEL_VMEM),
        name="finish",
    )(columns, pulled, resid)


def solution(mesh):
    placed = (P(None, "row", "col"), P(None, "row"), P(), P(), P("row", None, "col"))
    return jax.shard_map(
        on_device,
        mesh=mesh,
        in_specs=placed,
        out_specs=(P("row", None, "col"), P(None, "row", "col")),
        check_vma=False,
    )
```

time: 15.1 us -> 15 us (level)
  Pallas kernels: 14.3 us -> 14.1 us
where the time goes in v3:
time: 15 us; the launch traced here: 14.8 us
  Pallas kernels  14.1 us (94%)
  between operations  0.64 us (4%)
    pallas_call x1, Pallas kernels, on_device(): pl.pallas_call(functools.partial(exchange, rows, cols, 1.0 / math.sqrt(sl...  13 us
    pallas_call x1, Pallas kernels, on_device(): pl.pallas_call(finish, out_shape=(jax.ShapeDtypeStruct(measured.shape, f3...  1.14 us

profile of v3, /device:TPU:0, one launch (start us, length us, event | category | flops | bytes accessed | tf_op | source)
XLA Modules:
  0.0 14.8 jit_solution(9627428557458725011)
XLA Ops:
  0.6 13.0 %exchange.1 = (bf16[256,48]{1,0:T(8,128)(2,1)S(1)}, f32[2,64,128]{2,1,0:T(8,128)S(1)}, f32[2,16,128]{2,1,0:T(8,128)S(1)}) custom-call(f32[8,256,128]{2,1,0:T(8,128)} %volume_ref.1, f32[16,256]{1,0:T(8,128)} %weights_ref.1, bf16[16,128,128]{2,1,0:T(8,128)(2,1)} %shear_ref.1, s32[16]{0:T(128)} %offsets_ref.1, f32[4,8,128]{2,1,0:T(8,128)} %measured_ref.1), custom_call_target="tpu_custom_call" | custom-call | tf_op jit(solution)/shard_map/exchange/pallas_call | solution.py:386
  13.6 1.1 %finish.1 = (f32[4,8,128]{2,1,0:T(8,128)}, f32[8,256,128]{2,1,0:T(8,128)}) custom-call(bf16[256,48]{1,0:T(8,128)(2,1)S(1)} %get-tuple-element.5.columns_ref, f32[2,64,128]{2,1,0:T(8,128)S(1)} %get-tuple-element.6.pulled_ref, f32[2,16,128]{2,1,0:T(8,128)S(1)} %get-tuple-element.7.resid_ref), custom_call_target="tpu_custom_call" | custom-call | tf_op jit(solution)/shard_map/finish/pallas_call | solution.py:410

commit v4 on v3

--- a/solution.py
+++ b/solution.py
@@ -13,6 +13,7 @@
 KERNEL_VMEM = 24 * 1024 * 1024
 LATE_COLUMNS = 4
 HALVES = 2
+CHUNKS = 2
 
 
 def split(value):
@@ -114,17 +115,17 @@
     weights_copy.start()
     measured_copy = pltpu.make_async_copy(measured_ref, measured, local_sem.at[1])
     measured_copy.start()
-    volume_copies = []
-    for half in range(HALVES):
-        part = pl.ds(half * group, group)
-        copy = pltpu.make_async_copy(volume_ref.at[part], slab.at[part], slab_sem.at[half])
-        copy.start()
-        volume_copies.append(copy)
-
-    @pl.when(at_home)
-    def _():
-        others(lambda index, place: pl.semaphore_signal(barrier, inc=1, device_id=place, device_id_type=MESH),
-               last_first=True)
+    for chunk in range(HALVES * CHUNKS):
+        part = pl.ds(chunk * (group // CHUNKS), group // CHUNKS)
+        pltpu.make_async_copy(volume_ref.at[part], slab.at[part], slab_sem.at[chunk // CHUNKS]).start()
+
+    @pl.when(at_home)
+    def _():
+        def greet(index, place):
+            pl.semaphore_signal(barrier, inc=1, device_id=place, device_id_type=MESH)
+
+        others(greet, stop=2 * rows)
+        others(greet, stop=count - 1 - 2 * rows, last_first=True)
 
     def meet():
         @pl.when(at_home)
@@ -166,8 +167,7 @@
     weights = weights_in[...] * factor
     w_high, w_low = split(weights)
     w_both = jnp.concatenate([w_high, w_low], axis=0)
-    def send_tiles(halves):
-        order = homes.order
+    def send_tiles(halves, order=homes.order):
         rank = sum((mine == home).astype(jnp.int32) * turn for turn, home in enumerate(order))
         rank = lax.select(at_home, rank, jnp.int32(homes.count))
 
@@ -187,7 +187,8 @@
                 send_tile(half, homes.count - 1)
 
     for half in range(HALVES):
-        volume_copies[half].wait()
+        part = pl.ds(half * group, group)
+        pltpu.make_async_copy(volume_ref.at[part], slab.at[part], slab_sem.at[half]).wait()
         v_high, v_low = split(jnp.concatenate([slab[half * group + i] for i in range(group)], axis=1))
         first = jnp.dot(w_both, v_high, preferred_element_type=jnp.float32)
         second = jnp.dot(w_high, v_low, preferred_element_type=jnp.float32)
@@ -204,7 +205,7 @@
     @pl.when(jnp.logical_not(late))
     def _():
         meet()
-        send_tiles(range(HALVES))
+        send_tiles(range(HALVES), homes.order[::-1])
 
     pl.when(jnp.logical_not(late))(send_measured)
     shear_copy = pltpu.make_async_copy(shear_ref.at[pl.ds(mine * per, per)], shear, local_sem.at[0])
@@ -297,25 +298,33 @@
         level = jnp.concatenate([measure_in[c, half] for c in range(cols) for half in range(HALVES)], axis=0)
         spread = times(t_high, t_low, gains[0], gains[1]) - times(*split(level), gains[3])
         line = times(t_high, t_low, gains[2]) - level
-        for c in range(cols):
-            for half in range(HALVES):
-                at = (c * HALVES + half) * block
-                resid[c, half] = line[at:at + block]
-        for c in range(cols):
-            for half in range(HALVES):
-                at = (c * HALVES + half) * block
-                spreads[c, half] = spread[at:at + block]
-        for c in range(cols):
-            for half in range(HALVES):
-                pulls[c, half] = spreads[c, half]
-        for r in range(1, rows):
-            for c in range(cols):
+        tile = [[slice((c * HALVES + half) * block, (c * HALVES + half + 1) * block) for half in range(HALVES)]
+                for c in range(cols)]
+
+        def lay_pulls(c, rows_of):
+            for r in rows_of:
                 sources = [wrap(shifts[slot][r] + c, cols) for slot in range(per)]
                 for half in range(HALVES):
                     pulls[r * cols + c, half] = by_slot([spreads[source, half] for source in sources])
-        others(send_pull, stop=2)
+
+        for c in range(cols):
+            for half in range(HALVES):
+                spreads[c, half] = spread[tile[c][half]]
+        for half in range(HALVES):
+            pulls[0, half] = spread[tile[0][half]]
+        lay_pulls(0, range(1, rows))
+        early = min(2, rows - 1)
+        others(send_pull, stop=early)
+        for c in range(cols):
+            for half in range(HALVES):
+                resid[c, half] = line[tile[c][half]]
+        for c in range(1, cols):
+            for half in range(HALVES):
+                pulls[c, half] = spread[tile[c][half]]
+        for c in range(1, cols):
+            lay_pulls(c, range(1, rows))
         send_resid(0)
-        others(send_pull, start=2, stop=3 * rows)
+        others(send_pull, start=early, stop=3 * rows)
         each(cols - 2, lambda step: send_resid(step + 1))
         pl.when(jnp.logical_not(owned_here))(functools.partial(send_resid, cols - 1))
         others(send_pull, start=3 * rows)

time: 15 us -> 14.8 us (0.987)
    pallas_call x1, Pallas kernels: 13 us -> 12.8 us  [on_device(): pl.pallas_call(functools.partial(exchange, rows, cols, 1.0 / math.sqrt(sl...]
where the time goes in v4:
time: 14.8 us; the launch traced here: 14.6 us
  Pallas kernels  14 us (95%)
  between operations  0.64 us (4%)
    pallas_call x1, Pallas kernels, on_device(): pl.pallas_call(functools.partial(exchange, rows, cols, 1.0 / math.sqrt(sl...  12.8 us
    pallas_call x1, Pallas kernels, on_device(): pl.pallas_call(finish, out_shape=(jax.ShapeDtypeStruct(measured.shape, f3...  1.15 us

profile of v4, /device:TPU:0, one launch (start us, length us, event | category | flops | bytes accessed | tf_op | source)
XLA Modules:
  0.0 14.6 jit_solution(17986059764380565443)
XLA Ops:
  0.6 12.8 %exchange.1 = (bf16[256,48]{1,0:T(8,128)(2,1)S(1)}, f32[2,64,128]{2,1,0:T(8,128)S(1)}, f32[2,16,128]{2,1,0:T(8,128)S(1)}) custom-call(f32[8,256,128]{2,1,0:T(8,128)} %volume_ref.1, f32[16,256]{1,0:T(8,128)} %weights_ref.1, bf16[16,128,128]{2,1,0:T(8,128)(2,1)} %shear_ref.1, s32[16]{0:T(128)} %offsets_ref.1, f32[4,8,128]{2,1,0:T(8,128)} %measured_ref.1), custom_call_target="tpu_custom_call" | custom-call | tf_op jit(solution)/shard_map/exchange/pallas_call | solution.py:395
  13.5 1.1 %finish.1 = (f32[4,8,128]{2,1,0:T(8,128)}, f32[8,256,128]{2,1,0:T(8,128)}) custom-call(bf16[256,48]{1,0:T(8,128)(2,1)S(1)} %get-tuple-element.5.columns_ref, f32[2,64,128]{2,1,0:T(8,128)S(1)} %get-tuple-element.6.pulled_ref, f32[2,16,128]{2,1,0:T(8,128)S(1)} %get-tuple-element.7.resid_ref), custom_call_target="tpu_custom_call" | custom-call | tf_op jit(solution)/shard_map/finish/pallas_call | solution.py:419

commit v5 on v4

--- a/solution.py
+++ b/solution.py
@@ -68,7 +68,7 @@
     volume_ref, weights_ref, shear_ref, offsets_ref, measured_ref,
     columns_ref, pulled, resid_in,
     slab, weights_in, shear, gains, offsets, measured, leaving, tiles, landed, measure_in, resid, spreads, pulls,
-    slab_sem, local_sem, out_sem, in_sem, back_in_sem, m_out_sem, m_in_sem, r_in_sem,
+    slab_sem, out_sem, in_sem, back_in_sem, m_out_sem, m_in_sem, r_in_sem,
 ):
     slices = volume_ref.shape[0]
     angles = weights_ref.shape[0]
@@ -111,9 +111,9 @@
     block = per * group
     barrier = pltpu.get_barrier_semaphore()
 
-    weights_copy = pltpu.make_async_copy(weights_ref, weights_in, local_sem.at[0])
+    weights_copy = pltpu.make_async_copy(weights_ref, weights_in, out_sem)
     weights_copy.start()
-    measured_copy = pltpu.make_async_copy(measured_ref, measured, local_sem.at[1])
+    measured_copy = pltpu.make_async_copy(measured_ref, measured, m_out_sem)
     measured_copy.start()
     for chunk in range(HALVES * CHUNKS):
         part = pl.ds(chunk * (group // CHUNKS), group // CHUNKS)
@@ -208,9 +208,9 @@
         send_tiles(range(HALVES), homes.order[::-1])
 
     pl.when(jnp.logical_not(late))(send_measured)
-    shear_copy = pltpu.make_async_copy(shear_ref.at[pl.ds(mine * per, per)], shear, local_sem.at[0])
+    shear_copy = pltpu.make_async_copy(shear_ref.at[pl.ds(mine * per, per)], shear, slab_sem.at[0])
     shear_copy.start()
-    offsets_copy = pltpu.make_async_copy(offsets_ref, offsets, local_sem.at[1])
+    offsets_copy = pltpu.make_async_copy(offsets_ref, offsets, slab_sem.at[1])
     offsets_copy.start()
 
     columns_ref[...] = jnp.concatenate(
@@ -410,7 +410,7 @@
             pltpu.VMEM((HALVES, owned * group, width), f32),
             pltpu.VMEM((HALVES, angles * group, width), f32),
             halves(count), halves(cols), halves(cols), halves(cols), halves(count),
-            dma((HALVES,)), dma((2,)), dma, dma, dma, dma, dma, dma,
+            dma((HALVES,)), dma, dma, dma, dma, dma, dma,
         ],
         compiler_params=pltpu.CompilerParams(collective_id=0, has_side_effects=True, vmem_limit_bytes=KERNEL_VMEM),
         name="exchange",

time: 14.8 us -> 14.8 us (level)
  no operation moved by 1% of the time
where the time goes in v5:
time: 14.8 us; the launch traced here: 14.6 us
  Pallas kernels  14 us (95%)
  between operations  0.64 us (4%)
    pallas_call x1, Pallas kernels, on_device(): pl.pallas_call(functools.partial(exchange, rows, cols, 1.0 / math.sqrt(sl...  12.8 us
    pallas_call x1, Pallas kernels, on_device(): pl.pallas_call(finish, out_shape=(jax.ShapeDtypeStruct(measured.shape, f3...  1.15 us

profile of v5, /device:TPU:0, one launch (start us, length us, event | category | flops | bytes accessed | tf_op | source)
XLA Modules:
  0.0 14.6 jit_solution(12323249165089274905)
XLA Ops:
  0.6 12.8 %exchange.1 = (bf16[256,48]{1,0:T(8,128)(2,1)S(1)}, f32[2,64,128]{2,1,0:T(8,128)S(1)}, f32[2,16,128]{2,1,0:T(8,128)S(1)}) custom-call(f32[8,256,128]{2,1,0:T(8,128)} %volume_ref.1, f32[16,256]{1,0:T(8,128)} %weights_ref.1, bf16[16,128,128]{2,1,0:T(8,128)(2,1)} %shear_ref.1, s32[16]{0:T(128)} %offsets_ref.1, f32[4,8,128]{2,1,0:T(8,128)} %measured_ref.1), custom_call_target="tpu_custom_call" | custom-call | tf_op jit(solution)/shard_map/exchange/pallas_call | solution.py:395
  13.4 1.1 %finish.1 = (f32[4,8,128]{2,1,0:T(8,128)}, f32[8,256,128]{2,1,0:T(8,128)}) custom-call(bf16[256,48]{1,0:T(8,128)(2,1)S(1)} %get-tuple-element.5.columns_ref, f32[2,64,128]{2,1,0:T(8,128)S(1)} %get-tuple-element.6.pulled_ref, f32[2,16,128]{2,1,0:T(8,128)S(1)} %get-tuple-element.7.resid_ref), custom_call_target="tpu_custom_call" | custom-call | tf_op jit(solution)/shard_map/finish/pallas_call | solution.py:419

commit v6 on v5

--- a/solution.py
+++ b/solution.py
@@ -67,8 +67,8 @@
     rows, cols, factor, homes,
     volume_ref, weights_ref, shear_ref, offsets_ref, measured_ref,
     columns_ref, pulled, resid_in,
-    slab, weights_in, shear, gains, offsets, measured, leaving, tiles, landed, measure_in, resid, spreads, pulls,
-    slab_sem, out_sem, in_sem, back_in_sem, m_out_sem, m_in_sem, r_in_sem,
+    slab, weights_in, shear, gains, offsets, measured, leaving, tiles, landed, resid, spreads, pulls,
+    slab_sem, out_sem, in_sem, back_in_sem,
 ):
     slices = volume_ref.shape[0]
     angles = weights_ref.shape[0]
@@ -113,7 +113,7 @@
 
     weights_copy = pltpu.make_async_copy(weights_ref, weights_in, out_sem)
     weights_copy.start()
-    measured_copy = pltpu.make_async_copy(measured_ref, measured, m_out_sem)
+    measured_copy = pltpu.make_async_copy(measured_ref, measured, out_sem)
     measured_copy.start()
     for chunk in range(HALVES * CHUNKS):
         part = pl.ds(chunk * (group // CHUNKS), group // CHUNKS)
@@ -127,6 +127,10 @@
         others(greet, stop=2 * rows)
         others(greet, stop=count - 1 - 2 * rows, last_first=True)
 
+    def local_wait():
+        size = weights_ref.size + measured_ref.size
+        bytes_of(landed, size // (HALVES * block * width), out_sem).wait()
+
     def meet():
         @pl.when(at_home)
         def _():
@@ -137,7 +141,6 @@
             pl.semaphore_wait(barrier, homes.count)
 
     def send_measured():
-        measured_copy.wait()
         for s in range(slices):
             leaving[s // group, pl.ds(s % group, owned, stride=group), :] = measured[:, s, :]
         for r in range(rows):
@@ -147,23 +150,24 @@
                     place = homes.places[r * own_homes + k]
                     source = leaving.at[:, pl.ds(k * block, block)]
                     if place[0] != r:
-                        send(source, measure_in.at[col], m_out_sem, m_in_sem, place)
+                        send(source, landed.at[count + col], out_sem, in_sem, place)
                         continue
 
                     @pl.when(col != place[1])
                     def _():
-                        send(source, measure_in.at[col], m_out_sem, m_in_sem, place)
+                        send(source, landed.at[count + col], out_sem, in_sem, place)
 
                     @pl.when(col == place[1])
                     def _():
-                        measure_in[col] = leaving[:, k * block:(k + 1) * block]
+                        landed[count + col] = leaving[:, k * block:(k + 1) * block]
 
     @pl.when(late)
     def _():
         meet()
+        local_wait()
         send_measured()
 
-    weights_copy.wait()
+    pl.when(jnp.logical_not(late))(local_wait)
     weights = weights_in[...] * factor
     w_high, w_low = split(weights)
     w_both = jnp.concatenate([w_high, w_low], axis=0)
@@ -232,29 +236,11 @@
             gains[2, :, part] = shear[slot]
             gains[3, :, part] = shear[slot].T
 
-    @pl.when(at_home)
-    def _():
-        bytes_of(pulls, homes.count - 1, out_sem).wait()
-
-    @pl.when(away)
-    def _():
-        bytes_of(pulls, homes.count, out_sem).wait()
-
-    @pl.when(owner_here)
-    def _():
-        bytes_of(measure_in, own_homes - 1, m_out_sem).wait()
-
-    @pl.when(jnp.logical_not(owner_here))
-    def _():
-        bytes_of(measure_in, own_homes, m_out_sem).wait()
-
-    @pl.when(owner_here)
-    def _():
-        bytes_of(measure_in, cols - 1, m_in_sem).wait()
-
-    @pl.when(owner_there)
-    def _():
-        bytes_of(measure_in, cols, m_in_sem).wait()
+    def drained(ref, blocks, sem):
+        for case, fewer in ((away, 0), (owner_there, 1), (owner_here, 2)):
+            pl.when(case)(lambda fewer=fewer: bytes_of(ref, blocks - fewer, sem).wait())
+
+    drained(landed, homes.count + own_homes, out_sem)
 
     @pl.when(at_home)
     def _():
@@ -267,7 +253,7 @@
 
         def send_resid(step):
             c = step + (step >= lax.select(owned_here, col, jnp.int32(cols))).astype(jnp.int32)
-            send(resid.at[c], resid_in.at[:, first], m_out_sem, r_in_sem, (owner, c))
+            send(resid.at[c], resid_in.at[:, first], out_sem, back_in_sem, (owner, c))
 
         def by_slot(parts):
             chosen = parts[0]
@@ -285,7 +271,14 @@
         height = HALVES * cols * block
         slot_of = lax.rem(lax.broadcasted_iota(jnp.int32, (height, width), 0), block) // group
         shifts = [[wrap(offsets[mine * per + slot] * r, cols) for r in range(rows)] for slot in range(per)]
-        bytes_of(landed, count - 1, in_sem).wait()
+        @pl.when(owned_here)
+        def _():
+            bytes_of(landed, count - 1 + cols - 1, in_sem).wait()
+
+        @pl.when(jnp.logical_not(owned_here))
+        def _():
+            bytes_of(landed, count - 1 + cols, in_sem).wait()
+
         totals = []
         for c in range(cols):
             sources = [[wrap(cols - shifts[slot][r] + c, cols) for slot in range(per)] for r in range(rows)]
@@ -295,7 +288,7 @@
                     total = total + by_slot([landed[r * cols + sources[r][slot], half] for slot in range(per)])
                 totals.append(total)
         t_high, t_low = split(jnp.concatenate(totals, axis=0))
-        level = jnp.concatenate([measure_in[c, half] for c in range(cols) for half in range(HALVES)], axis=0)
+        level = jnp.concatenate([landed[count + c, half] for c in range(cols) for half in range(HALVES)], axis=0)
         spread = times(t_high, t_low, gains[0], gains[1]) - times(*split(level), gains[3])
         line = times(t_high, t_low, gains[2]) - level
         tile = [[slice((c * HALVES + half) * block, (c * HALVES + half + 1) * block) for half in range(HALVES)]
@@ -334,28 +327,15 @@
         def _():
             resid_in[:, first] = resid[col]
 
-        bytes_of(pulls, homes.count - 1, back_in_sem).wait()
-
-    @pl.when(away)
-    def _():
-        bytes_of(pulls, homes.count, back_in_sem).wait()
+    drained(landed, homes.count + own_homes, back_in_sem)
 
     @pl.when(owner_here)
     def _():
-        bytes_of(resid, own_homes - 1, r_in_sem).wait()
-        bytes_of(resid, cols - 1, m_out_sem).wait()
-
-    @pl.when(jnp.logical_not(owner_here))
-    def _():
-        bytes_of(resid, own_homes, r_in_sem).wait()
+        bytes_of(landed, count - 1 + cols - 1, out_sem).wait()
 
     @pl.when(owner_there)
     def _():
-        bytes_of(resid, cols, m_out_sem).wait()
-
-    @pl.when(at_home)
-    def _():
-        bytes_of(pulls, count - 1, out_sem).wait()
+        bytes_of(landed, count - 1 + cols, out_sem).wait()
 
 
 def finish(columns_ref, pulled_ref, resid_ref, residual_ref, gradient_ref, stage, natural, stage_sem, resid_sem):
@@ -409,8 +389,8 @@
             pltpu.VMEM(measured.shape, f32),
             pltpu.VMEM((HALVES, owned * group, width), f32),
             pltpu.VMEM((HALVES, angles * group, width), f32),
-            halves(count), halves(cols), halves(cols), halves(cols), halves(count),
-            dma((HALVES,)), dma, dma, dma, dma, dma, dma,
+            halves(count + cols), halves(cols), halves(cols), halves(count),
+            dma((HALVES,)), dma, dma, dma,
         ],
         compiler_params=pltpu.CompilerParams(collective_id=0, has_side_effects=True, vmem_limit_bytes=KERNEL_VMEM),
         name="exchange",

time: 14.8 us -> 14.8 us (level)
  no operation moved by 1% of the time
where the time goes in v6:
time: 14.8 us; the launch traced here: 14.6 us
  Pallas kernels  13.9 us (94%)
  between operations  0.64 us (4%)
    pallas_call x1, Pallas kernels, on_device(): pl.pallas_call(functools.partial(exchange, rows, cols, 1.0 / math.sqrt(sl...  12.8 us
    pallas_call x1, Pallas kernels, on_device(): pl.pallas_call(finish, out_shape=(jax.ShapeDtypeStruct(measured.shape, f3...  1.15 us

profile of v6, /device:TPU:0, one launch (start us, length us, event | category | flops | bytes accessed | tf_op | source)
XLA Modules:
  0.0 14.6 jit_solution(10927155741623925800)
XLA Ops:
  0.6 12.8 %exchange.1 = (bf16[256,48]{1,0:T(8,128)(2,1)S(1)}, f32[2,64,128]{2,1,0:T(8,128)S(1)}, f32[2,16,128]{2,1,0:T(8,128)S(1)}) custom-call(f32[8,256,128]{2,1,0:T(8,128)} %volume_ref.1, f32[16,256]{1,0:T(8,128)} %weights_ref.1, bf16[16,128,128]{2,1,0:T(8,128)(2,1)} %shear_ref.1, s32[16]{0:T(128)} %offsets_ref.1, f32[4,8,128]{2,1,0:T(8,128)} %measured_ref.1), custom_call_target="tpu_custom_call" | custom-call | tf_op jit(solution)/shard_map/exchange/pallas_call | solution.py:375
  13.4 1.1 %finish.1 = (f32[4,8,128]{2,1,0:T(8,128)}, f32[8,256,128]{2,1,0:T(8,128)}) custom-call(bf16[256,48]{1,0:T(8,128)(2,1)S(1)} %get-tuple-element.5.columns_ref, f32[2,64,128]{2,1,0:T(8,128)S(1)} %get-tuple-element.6.pulled_ref, f32[2,16,128]{2,1,0:T(8,128)S(1)} %get-tuple-element.7.resid_ref), custom_call_target="tpu_custom_call" | custom-call | tf_op jit(solution)/shard_map/finish/pallas_call | solution.py:399
